TPU v7x, 32 devices: a whole 2x2x4 slice. The times are simulated.
32 devices in a mesh: fsdp: 4 (over z), ctx: 4 (over y, x), tp: 2 (over core).
Axes of the slice: x: 2, y: 2, z: 4, core: 2. Of those that a mesh axis runs over, the one named last changes fastest.
Arguments:
- block_input: bfloat16 [4, 1024, 1600], P('fsdp', 'ctx'), may hold values from -8 to 8
- segments: int32 [4, 1024], P('fsdp', 'ctx'), may hold values from 0 to 3, never falling along the last dimension, each value on 1 to 512 neighbouring positions
- ln1_gain: float32 [1600], replicated, may hold values from 0.5 to 1.5
- ln1_shift: float32 [1600], replicated, may hold values from -3 to 3
- qkv_weight: bfloat16 [1600, 4800], P('fsdp'), may hold values from -4 to 4
- out_weight: bfloat16 [1600, 1600], P(None, 'fsdp'), may hold values from -0.4375 to 0.4375
- ln2_gain: float32 [1600], replicated, may hold values from 0.5 to 1.5
- ln2_shift: float32 [1600], replicated, may hold values from -3 to 3
- fc_weight: bfloat16 [1600, 6400], P('fsdp', 'tp'), may hold values from -0.15625 to 0.15625
- proj_weight: bfloat16 [6400, 1600], P('tp', 'fsdp'), may hold values from -0.078125 to 0.078125
- cotangent: bfloat16 [4, 1024, 1600], P('fsdp', 'ctx'), may hold values from -6 to 6
Outputs:
- block_output: bfloat16 [4, 1024, 1600], P('fsdp', 'ctx')
- grad_input: float32 [4, 1024, 1600], P('fsdp', 'ctx')
- grad_ln1_gain: float32 [1600], P(('fsdp', 'ctx'))
- grad_ln1_shift: float32 [1600], P(('fsdp', 'ctx'))
- grad_qkv_weight: float32 [1600, 4800], P(('fsdp', 'ctx'))
- grad_out_weight: float32 [1600, 1600], P(None, ('fsdp', 'ctx'))
- grad_ln2_gain: float32 [1600], P(('fsdp', 'ctx'))
- grad_ln2_shift: float32 [1600], P(('fsdp', 'ctx'))
- grad_fc_weight: float32 [1600, 6400], P(('fsdp', 'ctx'), 'tp')
- grad_proj_weight: float32 [6400, 1600], P('tp', ('fsdp', 'ctx'))
All inputs are finite; a program needn't handle non-finite values.
Results may differ from a plain program's by a relative error of at most 0.013.
The roundings to bfloat16 on the way count: a program that leaves them out, or rounds other values in their place, can miss the bound.
Values may be sent and summed in bfloat16 or wider, within the bound.
A program may use at most 320 MiB of HBM per device.

v0:
```python
import jax
import jax.numpy as jnp
from jax import lax
from jax.sharding import PartitionSpec as P

D = 1600
H = 25
HD = 64
norm_epsilon = 1e-05


def normalize(values, norm_gain, norm_shift):
    row_mean = jnp.mean(values, axis=-1, keepdims=True)
    centered = values - row_mean
    inv_std = lax.rsqrt(jnp.mean(centered * centered, axis=-1, keepdims=True) + norm_epsilon)
    normed = centered * inv_std
    return (normed * norm_gain + norm_shift, normed, inv_std)


def norm_back(upstream, normed, inv_std, norm_gain):
    scaled = upstream * norm_gain
    back_grad = inv_std * (
        scaled
        - jnp.mean(scaled, axis=-1, keepdims=True)
        - normed * jnp.mean(scaled * normed, axis=-1, keepdims=True)
    )
    return (back_grad, jnp.sum(upstream * normed, axis=(0, 1)), jnp.sum(upstream, axis=(0, 1)))


def masked_scores(queries, key_rows, query_seg, key_seg, query_pos):
    raw_scores = jnp.einsum("qhd,khd->hqk", queries, key_rows, preferred_element_type=jnp.float32)
    scores = raw_scores * queries.shape[-1] ** (-0.5)
    key_pos = jnp.arange(key_rows.shape[0], dtype=jnp.int32)
    allowed = (key_pos[None, :] <= query_pos[:, None]) & (key_seg[None, :] == query_seg[:, None])
    return jnp.where(allowed[None], scores, -1e30)


def attend(queries, key_rows, value_rows, query_seg, key_seg, query_pos):
    scores = masked_scores(queries, key_rows, query_seg, key_seg, query_pos)
    row_max = jnp.max(scores, axis=-1, keepdims=True)
    exponent = jnp.exp(scores - row_max)
    row_total = jnp.sum(exponent, axis=-1, keepdims=True)
    probabilities = (exponent / row_total).astype(jnp.bfloat16)
    attended = jnp.einsum(
        "hqk,khd->qhd", probabilities, value_rows, preferred_element_type=jnp.float32
    )
    return (attended, row_max + jnp.log(row_total))


def attend_back(
    queries, key_rows, value_rows, query_seg, key_seg, query_pos, log_total, grad_attended
):
    scores = masked_scores(queries, key_rows, query_seg, key_seg, query_pos)
    probabilities = jnp.exp(scores - log_total)
    grad_values = jnp.einsum(
        "hqk,qhd->khd",
        probabilities.astype(jnp.bfloat16),
        grad_attended,
        preferred_element_type=jnp.float32,
    )
    grad_probs = jnp.einsum(
        "qhd,khd->hqk", grad_attended, value_rows, preferred_element_type=jnp.float32
    )
    row_inner = jnp.sum(probabilities * grad_probs, axis=-1, keepdims=True)
    grad_raw = (probabilities * (grad_probs - row_inner) * queries.shape[-1] ** (-0.5)).astype(
        jnp.bfloat16
    )
    grad_query = jnp.einsum("hqk,khd->qhd", grad_raw, key_rows, preferred_element_type=jnp.float32)
    grad_keys = jnp.einsum("hqk,qhd->khd", grad_raw, queries, preferred_element_type=jnp.float32)
    return (grad_query, grad_keys, grad_values)


def slots_of(member, head_slots, tp_size):
    first_head = member * H // tp_size
    last_head = (member + 1) * H // tp_size
    wanted = first_head + jnp.arange(head_slots, dtype=jnp.int32)
    slot_heads = jnp.minimum(wanted, H - 1)
    slot_valid = (wanted < last_head).astype(jnp.float32)
    return (slot_heads, slot_valid)


def gelu_tanh(values):
    return jax.nn.gelu(values, approximate=True)


def local(
    block_input,
    segments,
    ln1_gain,
    ln1_shift,
    qkv_weight,
    out_weight,
    ln2_gain,
    ln2_shift,
    fc_weight,
    proj_weight,
    cotangent,
):
    tp_size = lax.axis_size("tp")
    tp_rank = lax.axis_index("tp")
    head_slots = (H + tp_size - 1) // tp_size
    slot_heads, slot_valid = slots_of(tp_rank, head_slots, tp_size)
    gathered = (
        lax.all_gather(qkv_weight, "fsdp", axis=0, tiled=True),
        lax.all_gather(out_weight, "fsdp", axis=1, tiled=True),
        lax.all_gather(fc_weight, "fsdp", axis=0, tiled=True),
        lax.all_gather(proj_weight, "fsdp", axis=1, tiled=True),
    )
    matrix = gathered[0]
    row_count = matrix.shape[0]
    query_key_value_weight = jnp.take(
        matrix.reshape(row_count, 3, H, HD), slot_heads, axis=2
    ).reshape(row_count, 3 * head_slots * HD)
    matrix = gathered[1]
    col_count = matrix.shape[1]
    contract_weight = jnp.take(matrix.reshape(H, HD, col_count), slot_heads, axis=0).reshape(
        head_slots * HD, col_count
    )
    expand_weight = gathered[2]
    attention_projection_weight = gathered[3]
    head_select_mask = jnp.repeat(slot_valid, HD).astype(jnp.bfloat16)
    contract_weight = contract_weight * head_select_mask[:, None]
    seq_count, local_len, model_width = block_input.shape
    input_f32 = block_input.astype(jnp.float32)
    hidden_one, normed_one, inv_one = normalize(input_f32, ln1_gain, ln1_shift)
    first_hidden_reduced = hidden_one.astype(jnp.bfloat16)
    qkv_values = jnp.einsum(
        "iwq,qr->iwr",
        first_hidden_reduced,
        query_key_value_weight,
        preferred_element_type=jnp.float32,
    ).astype(jnp.bfloat16)
    qkv_values = qkv_values.reshape(seq_count, local_len, 3, head_slots, HD)
    queries = qkv_values[:, :, 0]
    kv_local = jnp.stack([qkv_values[:, :, 1], qkv_values[:, :, 2]])
    seg_low = segments.astype(jnp.bfloat16)
    kv_all, seg_all = (
        lax.all_gather(kv_local, "ctx", axis=2, tiled=True),
        lax.all_gather(seg_low, "ctx", axis=1, tiled=True),
    )
    query_pos = lax.axis_index("ctx") * local_len + jnp.arange(local_len, dtype=jnp.int32)
    attended, log_total = lax.map(
        lambda entry: attend(entry[0], entry[1], entry[2], entry[3], entry[4], query_pos),
        (queries, kv_all[0], kv_all[1], seg_low, seg_all),
    )
    attention_output_reduced = attended.astype(jnp.bfloat16).reshape(
        seq_count, local_len, head_slots * HD
    )
    attn_sum = lax.psum(
        jnp.einsum(
            "qwa,ap->qwp",
            attention_output_reduced,
            contract_weight,
            preferred_element_type=jnp.float32,
        ),
        "tp",
    )
    residual_one = input_f32 + attn_sum
    hidden_two, normed_two, inv_two = normalize(residual_one, ln2_gain, ln2_shift)
    second_hidden_reduced = hidden_two.astype(jnp.bfloat16)
    pre_act = jnp.einsum(
        "whv,vi->whi", second_hidden_reduced, expand_weight, preferred_element_type=jnp.float32
    )
    activation, gelu_pull = jax.vjp(gelu_tanh, pre_act)
    activation_reduced = activation.astype(jnp.bfloat16)
    mlp_sum = lax.psum(
        jnp.einsum(
            "ojk,kg->ojg",
            activation_reduced,
            attention_projection_weight,
            preferred_element_type=jnp.float32,
        ).astype(jnp.bfloat16),
        "tp",
    ).astype(jnp.float32)
    result = (residual_one + mlp_sum).astype(jnp.bfloat16)
    grad_output = cotangent.astype(jnp.float32)
    projection_gradient = jnp.einsum(
        "xbi,xbm->im", activation_reduced, cotangent, preferred_element_type=jnp.float32
    )
    activation_gradient = jnp.einsum(
        "tua,ya->tuy", cotangent, attention_projection_weight, preferred_element_type=jnp.float32
    )
    preactivation_gradient = gelu_pull(activation_gradient)[0].astype(jnp.bfloat16)
    grad_fc = jnp.einsum(
        "atm,atk->mk",
        second_hidden_reduced,
        preactivation_gradient,
        preferred_element_type=jnp.float32,
    )
    grad_h2 = lax.psum(
        jnp.einsum(
            "kau,gu->kag", preactivation_gradient, expand_weight, preferred_element_type=jnp.float32
        ),
        "tp",
    )
    back_two, grad_g2, grad_s2 = norm_back(grad_h2, normed_two, inv_two, ln2_gain)
    grad_r1 = grad_output + back_two
    attention_gradient = grad_r1.astype(jnp.bfloat16)
    grad_out_local = jnp.einsum(
        "izy,izr->yr",
        attention_output_reduced * head_select_mask,
        attention_gradient,
        preferred_element_type=jnp.float32,
    )
    grad_attended = jnp.einsum(
        "gmi,ti->gmt", attention_gradient, contract_weight, preferred_element_type=jnp.float32
    )
    grad_attended = grad_attended.astype(jnp.bfloat16).reshape(seq_count, local_len, head_slots, HD)
    grad_query, grad_keys, grad_values = lax.map(
        lambda entry: attend_back(
            entry[0], entry[1], entry[2], entry[3], entry[4], query_pos, entry[5], entry[6]
        ),
        (queries, kv_all[0], kv_all[1], seg_low, seg_all, log_total, grad_attended),
    )
    kv_grad = lax.psum_scatter(
        jnp.stack([grad_keys, grad_values]).astype(jnp.bfloat16),
        "ctx",
        scatter_dimension=2,
        tiled=True,
    ).astype(jnp.float32)
    query_key_value_gradient = jnp.stack([grad_query, kv_grad[0], kv_grad[1]], axis=2).astype(
        jnp.bfloat16
    )
    query_key_value_gradient = query_key_value_gradient.reshape(
        seq_count, local_len, 3 * head_slots * HD
    )
    grad_qkv_local = jnp.einsum(
        "axy,axh->yh",
        first_hidden_reduced,
        query_key_value_gradient,
        preferred_element_type=jnp.float32,
    )
    grad_h1 = lax.psum(
        jnp.einsum(
            "cbz,iz->cbi",
            query_key_value_gradient,
            query_key_value_weight,
            preferred_element_type=jnp.float32,
        ),
        "tp",
    )
    back_one, grad_g1, grad_s1 = norm_back(grad_h1, normed_one, inv_one, ln1_gain)
    grad_total = grad_r1 + back_one
    qkv_full = (
        jnp.zeros((D, 3, H, HD), jnp.float32)
        .at[:, :, slot_heads, :]
        .add(grad_qkv_local.reshape(D, 3, head_slots, HD))
    )
    out_full = (
        jnp.zeros((H, HD, D), jnp.float32)
        .at[slot_heads]
        .add(grad_out_local.reshape(head_slots, HD, D))
    )
    partial_value = (
        lax.psum_scatter(
            qkv_full.reshape(D, 3 * H * HD), ("fsdp", "ctx"), scatter_dimension=0, tiled=True
        ),
        lax.psum_scatter(
            out_full.reshape(H * HD, D), ("fsdp", "ctx"), scatter_dimension=1, tiled=True
        ),
    )
    qkv_grad_out, out_grad_out = (
        lax.psum(partial_value[0].astype(jnp.bfloat16), "tp").astype(jnp.float32),
        lax.psum(partial_value[1].astype(jnp.bfloat16), "tp").astype(jnp.float32),
    )
    unit_sums = (
        lax.psum_scatter(grad_fc, ("fsdp", "ctx"), scatter_dimension=0, tiled=True),
        lax.psum_scatter(projection_gradient, ("fsdp", "ctx"), scatter_dimension=1, tiled=True),
        lax.psum_scatter(grad_g1, ("fsdp", "ctx"), scatter_dimension=0, tiled=True),
        lax.psum_scatter(grad_s1, ("fsdp", "ctx"), scatter_dimension=0, tiled=True),
        lax.psum_scatter(grad_g2, ("fsdp", "ctx"), scatter_dimension=0, tiled=True),
        lax.psum_scatter(grad_s2, ("fsdp", "ctx"), scatter_dimension=0, tiled=True),
    )
    return (
        result,
        grad_total,
        unit_sums[2],
        unit_sums[3],
        qkv_grad_out,
        out_grad_out,
        unit_sums[4],
        unit_sums[5],
        unit_sums[0],
        unit_sums[1],
    )


def solution(mesh):
    placed = (
        P("fsdp", "ctx", None),
        P("fsdp", "ctx"),
        P(),
        P(),
        P("fsdp", None),
        P(None, "fsdp"),
        P(),
        P(),
        P("fsdp", "tp"),
        P("tp", "fsdp"),
        P("fsdp", "ctx", None),
    )
    return jax.shard_map(
        local,
        mesh=mesh,
        in_specs=placed,
        out_specs=(
            P("fsdp", "ctx", None),
            P("fsdp", "ctx", None),
            P(("fsdp", "ctx")),
            P(("fsdp", "ctx")),
            P(("fsdp", "ctx"), None),
            P(None, ("fsdp", "ctx")),
            P(("fsdp", "ctx")),
            P(("fsdp", "ctx")),
            P(("fsdp", "ctx"), "tp"),
            P("tp", ("fsdp", "ctx")),
        ),
        check_vma=False,
    )
```

profile of v0, /device:TPU:0, one launch (start us, length us, event | category | flops | bytes accessed | tf_op | source)
XLA Modules:
  0.0 3262.2 jit_solution(14725272297948683888)
XLA Ops:
  9.3 269.9 %all-gather.6.cloned.1.call-done = bf16[1600,4800]{1,0:T(8,128)(2,1)} async-done(((bf16[400,4800]{1,0:T(8,128)(2,1)}), bf16[1600,4800]{1,0:T(8,128)(2,1)}) %all-gather.6.cloned.1.call-update) | async-done | bytes 15360016 | tf_op jit(solution)/shard_map/all_gather | solution.py:104
  279.3 22.4 copy.30
  301.6 13.5 copy.31
  315.1 10.7 gather_fusion
  348.0 8.2 all_gather.22
  356.6 21.8 all-gather.10.cloned.1.call-done
  378.4 9.6 copy.33
  396.9 28.2 all-gather.8.cloned.1.call-done
  453.8 16.0 all-reduce.20.cloned.1.call-done
  471.8 180.5 %all-gather.12.cloned.1.call-done = bf16[1600,3200]{1,0:T(8,128)(2,1)} async-done(((bf16[400,3200]{1,0:T(8,128)(2,1)}), bf16[1600,3200]{1,0:T(8,128)(2,1)}) %all-gather.12.cloned.1.call-update) | async-done | bytes 10240016 | tf_op jit(solution)/shard_map/all_gather | solution.py:106
  652.3 9.1 fusion.86
  661.4 170.5 %all-gather.14.cloned.1.call-done = bf16[3200,1600]{0,1:T(8,128)(2,1)} async-done(((bf16[3200,400]{0,1:T(8,128)(2,1)}), bf16[3200,1600]{0,1:T(8,128)(2,1)}) %all-gather.14.cloned.1.call-update) | async-done | bytes 10240016 | tf_op jit(solution)/shard_map/all_gather | solution.py:107
  831.8 9.8 fusion.26
  847.3 10.8 fusion.66
  858.1 9.2 fusion.84
  873.7 8.5 fusion.48
  889.0 26.9 fusion.51
  920.1 961.2 %fusion.88 = (f32[112,3200]{1,0:T(8,128)}, f32[3200,112]{0,1:T(8,128)S(1)}) fusion(f32[1600,3200]{1,0:T(8,128)} %fusion.84, f32[3200,1600]{0,1:T(8,128)} %fusion.66), kind=kCustom, calls=%all-reduce-scatter.3 | all-reduce-scatter fusion | flops 11468801 | bytes 43827712
  1894.3 25.5 fusion.55
  1921.2 8.4 convolution_bitcast_fusion
  1929.6 7.9 convolution_bitcast_fusion.1
  1937.6 11.4 copy.34
  1949.0 10.9 broadcast_in_dim.115
  1960.0 33.4 %scatter_fusion = f32[1600,3,25,64]{0,3,2,1:T(8,128)} fusion(f32[1600,3,25,64]{0,3,2,1:T(8,128)} %broadcast_in_dim.115, s32[13]{0:T(128)S(1)} %copy-done.27, f32[13,1600,3,64]{1,3,2,0:T(8,128)} %copy.34), kind=kCustom, calls=%fused_computation.2 | custom fusion | flops 3993600 | bytes 47923252 | tf_op jit(solution)/shard_map/scatter-add | solution.py:247
  1993.4 34.2 %copy.35 = f32[1600,4800]{1,0:T(8,128)} copy(f32[1600,4800]{0,1:T(8,128)} %bitcast.129) | data formatting | bytes 61440000 | tf_op jit(solution)/shard_map/reshape | solution.py:256
  2027.6 671.4 %fusion = f32[104,4800]{1,0:T(8,128)} fusion(f32[1600,4800]{1,0:T(8,128)} %copy.35), kind=kCustom, calls=%all-reduce-scatter | all-reduce-scatter fusion | flops 7987201 | bytes 32717312
  2702.9 8.9 fusion.27
  2720.3 15.3 scatter_fusion.1
  2735.6 9.3 concatenate.17
  2749.8 459.8 %all-reduce.27 = (bf16[1600,1600]{1,0:T(8,128)(2,1)}, f32[1600]{0:T(1024)S(1)}, f32[1600]{0:T(1024)S(1)}, f32[1600]{0:T(1024)S(1)}, f32[1600]{0:T(1024)S(1)}) all-reduce(f32[1600,1600]{1,0:T(8,128)} %bitcast.130, f32[1600]{0:T(1024)S(1)} %get-tuple-element.95, ...), channel_id=6, replica_groups=mesh['fsdp'=4,'ctx'=4,'tp'=2] {'fsdp','ctx'}, use_global_device_ids=true, to_apply=%region_24.25.clone | all-reduce | flops 2566400 | bytes 15411200
  3212.3 14.7 concatenate.18
  3227.0 13.9 concatenate.19
  (156 shorter events, 133.5 us)
Async XLA Ops:
  7.2 272.1 %all-gather.6.cloned.1.call-start = ((), (), s32[]{:S(2)}) async-start(), calls=%async_computation.1 | async-start | bytes 19456000 | tf_op jit(solution)/shard_map/all_gather | solution.py:104
  7.9 370.5 %all-gather.10.cloned.1.call-start = ((), (), s32[]{:S(2)}) async-start(), calls=%async_computation.3 | async-start | bytes 6656000 | tf_op jit(solution)/shard_map/all_gather | solution.py:105
  8.7 416.4 %all-gather.8.cloned.1.call-start = ((), (), s32[]{:S(2)}) async-start(), calls=%async_computation.2 | async-start | bytes 4259840 | tf_op jit(solution)/shard_map/all_gather | solution.py:138
  8.7 292.9 %copy-start.26 = (s32[13]{0:T(128)}, s32[13]{0:T(128)S(1)}, u32[]{:S(2)}) copy-start(s32[13]{0:T(128)S(1)} %fusion.77) | copy-start | bytes 160
  333.3 7.3 copy-start.22
  333.3 7.3 copy-start.25
  346.6 78.5 %copy-start.17 = (bf16[256,2496]{0,1:T(8,128)(2,1)}, bf16[256,2496]{0,1:T(8,128)(2,1)S(1)}, u32[]{:S(2)}) copy-start(bf16[256,2496]{0,1:T(8,128)(2,1)S(1)} %convolution_convert_fusion) | copy-start | bytes 3833860
  347.9 121.9 %all-reduce.20.cloned.1.call-start = ((), (), s32[]{:S(2)}) async-start(), calls=%async_computation.4 | async-start | bytes 3276800 | tf_op jit(solution)/shard_map/psum | solution.py:149
  432.7 7.3 copy-start.12
  449.1 203.1 %all-gather.12.cloned.1.call-start = ((), (), s32[]{:S(2)}) async-start(), calls=%async_computation.5 | async-start | bytes 12800000 | tf_op jit(solution)/shard_map/all_gather | solution.py:106
  449.7 382.1 %all-gather.14.cloned.1.call-start = ((), (), s32[]{:S(2)}) async-start(), calls=%async_computation.6 | async-start | bytes 12800000 | tf_op jit(solution)/shard_map/all_gather | solution.py:107
  450.3 417.0 %all-reduce.22.cloned.1.call-start = ((), (), s32[]{:S(2)}) async-start(), calls=%async_computation.7 | async-start | bytes 3276800 | tf_op jit(solution)/shard_map/psum | solution.py:190
  452.8 199.4 %copy-start.19 = (f32[1600]{0:T(1024)S(1)}, f32[1600]{0:T(1024)}, u32[]{:S(2)}) copy-start(f32[1600]{0:T(1024)} %param.17) | copy-start | bytes 19204
  452.8 199.4 %copy-start.21 = (f32[1600]{0:T(1024)S(1)}, f32[1600]{0:T(1024)}, u32[]{:S(2)}) copy-start(f32[1600]{0:T(1024)} %param.18) | copy-start | bytes 19204
  471.5 398.9 %copy-start = (f32[1,256,1600]{1,2,0:T(8,128)}, f32[1,256,1600]{1,2,0:T(8,128)S(1)}, u32[]{:S(2)}) copy-start(f32[1,256,1600]{1,2,0:T(8,128)S(1)} %get-tuple-element.114) | copy-start | bytes 4915204
  471.7 360.1 %copy-start.11 = (bf16[1,256,1600]{1,2,0:T(8,128)(2,1)S(1)}, bf16[1,256,1600]{1,2,0:T(8,128)(2,1)}, u32[]{:S(2)}) copy-start(bf16[1,256,1600]{1,2,0:T(8,128)(2,1)} %param.21) | copy-start | bytes 2457604
  831.8 11.0 copy-start.3
  847.0 1072.8 %reduce-scatter.9.cloned.1.call-start = ((), (), s32[]{:S(2)}) async-start(), calls=%async_computation.8 | async-start | bytes 4259840 | tf_op jit(solution)/shard_map/reduce_scatter | solution.py:215
  847.3 10.9 copy-start.16
  873.7 8.5 copy-start.13
  920.1 1827.3 %all-reduce.24.cloned.1.call-start = ((), (), s32[]{:S(2)}) async-start(), calls=%async_computation.9 | async-start | bytes 3276800 | tf_op jit(solution)/shard_map/psum | solution.py:233
  1883.5 1328.8 %collective-permute-start.1 = (f32[112,3200]{1,0:T(8,128)}, f32[112,3200]{1,0:T(8,128)}, u32[]{:S(2)}, u32[]{:S(2)}) collective-permute-start(f32[112,3200]{1,0:T(8,128)} %get-tuple-element.111), channel_id=1, source_target_pairs={{0,2},{2,4},{4,6},{6,8},{8,10},{10,12},{12,14},{14,16},{16,18},{18... | collective-permute-start | bytes 4300808
  1887.0 1340.0 %collective-permute-start.3 = (f32[3200,112]{0,1:T(8,128)S(1)}, f32[3200,112]{0,1:T(8,128)}, u32[]{:S(2)}, u32[]{:S(2)}) collective-permute-start(f32[3200,112]{0,1:T(8,128)S(1)} %get-tuple-element.112), channel_id=1, source_target_pairs={{0,2},{2,4},{4,6},{6,8},{8,10},{10,12},{12,14},{14,16},{16,18},{18... | collective-permute-start | bytes 4300808
  1889.4 1337.6 %collective-permute-start.4 = (f32[3200,68]{0,1:T(8,128)}, f32[3200,68]{0,1:T(8,128)}, u32[]{:S(2)}, u32[]{:S(2)}) collective-permute-start(f32[3200,68]{0,1:T(8,128)} %slice.43), channel_id=1, source_target_pairs={{0,4},{2,6},{4,8},{6,10},{8,12},{10,14},{12,16},{14,18},{16,20},{1... | collective-permute-start | bytes 2611208
  1892.1 1320.2 %collective-permute-start.2 = (f32[68,3200]{1,0:T(8,128)}, f32[68,3200]{1,0:T(8,128)}, u32[]{:S(2)}, u32[]{:S(2)}) collective-permute-start(f32[68,3200]{1,0:T(8,128)} %slice.42), channel_id=1, source_target_pairs={{0,4},{2,6},{4,8},{6,10},{8,12},{10,14},{12,16},{14,18},{16,20},{1... | collective-permute-start | bytes 2611208
  1937.6 1312.5 %all-reduce.26.cloned.1.call-start = ((), (), s32[]{:S(2)}) async-start(), calls=%async_computation.10 | async-start | bytes 4481024 | tf_op jit(solution)/shard_map/psum | solution.py:264
  1949.0 11.0 copy-start.27
  2701.2 10.6 copy-start.5
  2701.2 10.6 copy-start.14
  2701.2 34.4 %collective-permute-start = (bf16[60,4800]{1,0:T(8,128)(2,1)}, bf16[60,4800]{1,0:T(8,128)(2,1)S(1)}, u32[]{:S(2)}, u32[]{:S(2)}) collective-permute-start(bf16[60,4800]{1,0:T(8,128)(2,1)} %slice.41), channel_id=1, source_target_pairs={{0,2},{2,4},{4,6},{6,8},{8,10},{10,12},{12,14},{14,16},{16,18},{18... | collective-permute-start | bytes 1728008
  3240.9 7.6 copy-start.6
  3240.9 7.6 copy-start.9
  (13 other events, 40.1 us)
Sparse Core Ops, SparseCore 0:
  9.6 269.6 all-gather.5
  280.8 97.5 all-gather.9
  380.8 44.2 all-gather.7
  449.3 20.4 all-reduce.19
  471.2 181.0 all-gather.11
  653.7 178.0 all-gather.13
  847.2 18.6 all-reduce.21
  920.2 149.3 reduce-scatter.8
  1937.7 32.3 all-reduce.23
  3211.8 20.5 all-reduce.25
where the time goes:
time: 3270 us; the launch traced here: 3260 us
  blocking collectives  2100 us (64%)
  waiting for transfers between devices  689 us (21%)
  local copies, waits for them, and re-layouts  192 us (6%)
  matrix products  163 us (5%)
  other arithmetic  87.7 us (3%)
    unnamed x3, blocking collectives  2090 us
    all_gather x1, waiting for transfers between devices, local(): lax.all_gather(qkv_weight, 'fsdp', axis=0, tiled=True)  270 us
    all_gather x1, waiting for transfers between devices, local(): lax.all_gather(fc_weight, 'fsdp', axis=0, tiled=True)  181 us
    all_gather x1, waiting for transfers between devices, local(): lax.all_gather(proj_weight, 'fsdp', axis=1, tiled=True)  170 us
  transfers between devices with their start and end apart: 15, of which 6 were waited for; matrix products, arithmetic and copies ran while one was open for 61% of the time, Pallas kernels for 0%

commit v1 on v0

--- a/solution.py
+++ b/solution.py
@@ -7,6 +7,24 @@
 H = 25
 HD = 64
 norm_epsilon = 1e-05
+
+
+def gather_around(array, axis, dim):
+    ways, here, step = (lax.axis_size(axis), lax.axis_index(axis), array.shape[dim])
+    shape = [n * ways if d == dim else n for d, n in enumerate(array.shape)]
+    full = lax.dynamic_update_slice_in_dim(
+        jnp.zeros(shape, array.dtype), array, here * step, axis=dim
+    )
+    going_up = going_down = array
+    for far in range(1, ways // 2 + 1):
+        going_up = lax.ppermute(going_up, axis, [(d, (d + 1) % ways) for d in range(ways)])
+        full = lax.dynamic_update_slice_in_dim(full, going_up, (here - far) % ways * step, axis=dim)
+        if 2 * far < ways:
+            going_down = lax.ppermute(going_down, axis, [(d, (d - 1) % ways) for d in range(ways)])
+            full = lax.dynamic_update_slice_in_dim(
+                full, going_down, (here + far) % ways * step, axis=dim
+            )
+    return full
 
 
 def normalize(values, norm_gain, norm_shift):
@@ -104,7 +122,7 @@
         lax.all_gather(qkv_weight, "fsdp", axis=0, tiled=True),
         lax.all_gather(out_weight, "fsdp", axis=1, tiled=True),
         lax.all_gather(fc_weight, "fsdp", axis=0, tiled=True),
-        lax.all_gather(proj_weight, "fsdp", axis=1, tiled=True),
+        gather_around(proj_weight, "fsdp", 1),
     )
     matrix = gathered[0]
     row_count = matrix.shape[0]

time: 3270 us -> 3310 us (1.012)
  waiting for transfers between devices: 689 us -> 617 us
  starting transfers between devices: 12.5 us -> 81.6 us
    ppermute x0 -> x3, waiting for transfers between devices: none -> 229 us  [the longest x2 125 us: gather_around(): lax.ppermute(going_up, axis, [(d, (d + 1) % ways) for d in range(ways)])]
    all_gather x1 -> x0, waiting for transfers between devices: 170 us -> none  [local(): lax.all_gather(proj_weight, 'fsdp', axis=1, tiled=True)]
    all_gather x1, waiting for transfers between devices: 181 us -> 25.4 us  [local(): lax.all_gather(fc_weight, 'fsdp', axis=0, tiled=True)]
    ppermute x0 -> x3, starting transfers between devices: none -> 58.2 us  [the longest x2 55.9 us: gather_around(): lax.ppermute(going_up, axis, [(d, (d + 1) % ways) for d in range(ways)])]
    psum x1, waiting for transfers between devices: 0.01 us -> 39.7 us  [local(): lax.psum(partial_value[1].astype(jnp.bfloat16), 'tp').astype(jnp.float32)]
  transfers between devices with their start and end apart: 15 -> 17, of which waited for: 6 -> 9; matrix products, arithmetic and copies ran while one was open for 61% -> 60% of each run, Pallas kernels for 0% -> 0%
where the time goes in v1:
time: 3310 us; the launch traced here: 3290 us
  blocking collectives  2120 us (64%)
  waiting for transfers between devices  617 us (19%)
  local copies, waits for them, and re-layouts  209 us (6%)
  matrix products  163 us (5%)
  other arithmetic  87.7 us (3%)
  starting transfers between devices  81.6 us (2%)
    unnamed x3, blocking collectives  2110 us
    all_gather x1, waiting for transfers between devices, local(): lax.all_gather(qkv_weight, 'fsdp', axis=0, tiled=True)  270 us
    ppermute x2, waiting for transfers between devices, gather_around(): lax.ppermute(going_up, axis, [(d, (d + 1) % ways) for d in range(ways)])  125 us
    ppermute x1, waiting for transfers between devices, gather_around(): lax.ppermute(going_down, axis, [(d, (d - 1) % ways) for d in range(ways)])  104 us
  transfers between devices with their start and end apart: 17, of which 9 were waited for; matrix products, arithmetic and copies ran while one was open for 60% of the time, Pallas kernels for 0%

profile of v1, /device:TPU:0, one launch (start us, length us, event | category | flops | bytes accessed | tf_op | source)
XLA Modules:
  0.0 3289.9 jit_solution(9248484667686018520)
XLA Ops:
  9.3 269.9 %all-gather.5.cloned.1.call-done = bf16[1600,4800]{1,0:T(8,128)(2,1)} async-done(((bf16[400,4800]{1,0:T(8,128)(2,1)}), bf16[1600,4800]{1,0:T(8,128)(2,1)}) %all-gather.5.cloned.1.call-update) | async-done | bytes 15360016 | tf_op jit(solution)/shard_map/all_gather | solution.py:122
  279.3 22.4 copy.32
  301.7 13.5 copy.33
  315.2 10.7 gather_fusion
  356.8 21.6 all-gather.9.cloned.1.call-done
  378.4 9.4 copy.35
  396.9 28.2 all-gather.7.cloned.1.call-done
  453.7 80.1 %collective-permute-done = bf16[3200,400]{0,1:T(8,128)(2,1)} collective-permute-done((bf16[3200,400]{0,1:T(8,128)(2,1)}, bf16[3200,400]{0,1:T(8,128)(2,1)}, u32[]{:S(2)}, u32[]{:S(2)}) %collective-permute-start) | collective-permute-done | bytes 2560032 | tf_op jit(solution)/shard_map/ppermute | solution.py:20
  533.8 54.3 %collective-permute-start.2 = (bf16[3200,400]{0,1:T(8,128)(2,1)}, bf16[3200,400]{0,1:T(8,128)(2,1)}, u32[]{:S(2)}, u32[]{:S(2)}) collective-permute-start(bf16[3200,400]{0,1:T(8,128)(2,1)} %collective-permute-done), channel_id=1, source_target_pairs={{0,8},{8,16},{16,24},{24,0},{1,9},{9,17},{17,25},{25,1},{2,10},{10... | collective-permute-start | bytes 7680008 | tf_op jit(solution)/shard_map/ppermute | solution.py:20
  599.8 104.0 %collective-permute-done.1 = bf16[3200,400]{0,1:T(8,128)(2,1)} collective-permute-done((bf16[3200,400]{0,1:T(8,128)(2,1)}, bf16[3200,400]{0,1:T(8,128)(2,1)}, u32[]{:S(2)}, u32[]{:S(2)}) %collective-permute-start.1) | collective-permute-done | bytes 2560032 | tf_op jit(solution)/shard_map/ppermute | solution.py:23
  707.2 44.8 %collective-permute-done.2 = bf16[3200,400]{0,1:T(8,128)(2,1)} collective-permute-done((bf16[3200,400]{0,1:T(8,128)(2,1)}, bf16[3200,400]{0,1:T(8,128)(2,1)}, u32[]{:S(2)}, u32[]{:S(2)}) %collective-permute-start.2) | collective-permute-done | bytes 2560032 | tf_op jit(solution)/shard_map/ppermute | solution.py:20
  758.3 25.4 all-gather.11.cloned.1.call-done
  791.3 10.4 fusion.26
  807.4 11.1 fusion.66
  818.4 9.2 fusion.81
  835.5 8.5 fusion.48
  850.8 26.8 fusion.51
  881.8 961.2 %fusion.85 = (f32[112,3200]{1,0:T(8,128)}, f32[3200,112]{0,1:T(8,128)S(1)}) fusion(f32[1600,3200]{1,0:T(8,128)} %fusion.81, f32[3200,1600]{0,1:T(8,128)} %fusion.66), kind=kCustom, calls=%all-reduce-scatter.3 | all-reduce-scatter fusion | flops 11468801 | bytes 43827712
  1843.0 25.5 fusion.55
  1886.2 11.4 copy.37
  1897.6 10.8 broadcast_in_dim.119
  1908.4 33.6 %scatter_fusion = f32[1600,3,25,64]{0,3,2,1:T(8,128)} fusion(f32[1600,3,25,64]{0,3,2,1:T(8,128)} %broadcast_in_dim.119, s32[13]{0:T(128)S(1)} %copy-done.28, f32[13,1600,3,64]{1,3,2,0:T(8,128)} %copy.37), kind=kCustom, calls=%fused_computation.2 | custom fusion | flops 3993600 | bytes 47923252 | tf_op jit(solution)/shard_map/scatter-add | solution.py:265
  1942.0 34.2 %copy.38 = f32[1600,4800]{1,0:T(8,128)} copy(f32[1600,4800]{0,1:T(8,128)} %bitcast.131) | data formatting | bytes 61440000 | tf_op jit(solution)/shard_map/reshape | solution.py:274
  1976.1 660.8 %fusion = f32[104,4800]{1,0:T(8,128)} fusion(f32[1600,4800]{1,0:T(8,128)} %copy.38), kind=kCustom, calls=%all-reduce-scatter | all-reduce-scatter fusion | flops 7987201 | bytes 32717312
  2641.6 8.9 fusion.27
  2661.2 13.2 collective-permute-start.5
  2683.0 15.2 scatter_fusion.1
  2698.1 11.6 concatenate.17
  2714.5 485.5 %all-reduce.27 = (bf16[1600,1600]{1,0:T(8,128)(2,1)}, f32[1600]{0:T(1024)S(1)}, f32[1600]{0:T(1024)S(1)}, f32[1600]{0:T(1024)S(1)}, f32[1600]{0:T(1024)S(1)}) all-reduce(f32[1600,1600]{1,0:T(8,128)} %bitcast.132, f32[1600]{0:T(1024)S(1)} %get-tuple-element.95, ...), channel_id=6, replica_groups=mesh['fsdp'=4,'ctx'=4,'tp'=2] {'fsdp','ctx'}, use_global_device_ids=true, to_apply=%region_24.25.clone | all-reduce | flops 2566400 | bytes 15411200
  3202.7 14.5 concatenate.18
  3217.3 12.1 concatenate.19
  3238.7 39.7 %all-reduce.26.cloned.1.call-done = (bf16[1600,100]{1,0:T(8,128)(2,1)}, bf16[1,256,1600]{1,2,0:T(8,128)(2,1)}, bf16[100,4800]{1,0:T(8,128)(2,1)}) async-done(((bf16[1600,100]{1,0:T(8,128)(2,1)}, bf16[1,256,1600]{1,2,0:T(8,128)(2,1)}, bf16[100,4800]{1,0:T(8,128)(2,1)}), (bf16[1600,100]{1,0:T(8,128)(2,1)}, bf16[1,256,1600]{1,2,0:T(8,128)(2,1)}, bf16[100,4800]{1,0:T(8,128)(2,1)})) %all-reduce.26.cloned.1.call-update) | async-done | bytes 2099216 | tf_op jit(solution)/shard_map/psum | solution.py:282
  (173 shorter events, 185.2 us)
Async XLA Ops:
  7.2 272.1 %all-gather.5.cloned.1.call-start = ((), (), s32[]{:S(2)}) async-start(), calls=%async_computation.1 | async-start | bytes 19456000 | tf_op jit(solution)/shard_map/all_gather | solution.py:122
  7.9 370.5 %all-gather.9.cloned.1.call-start = ((), (), s32[]{:S(2)}) async-start(), calls=%async_computation.3 | async-start | bytes 6656000 | tf_op jit(solution)/shard_map/all_gather | solution.py:123
  8.7 416.4 %all-gather.7.cloned.1.call-start = ((), (), s32[]{:S(2)}) async-start(), calls=%async_computation.2 | async-start | bytes 4259840 | tf_op jit(solution)/shard_map/all_gather | solution.py:156
  8.7 292.9 %copy-start.27 = (s32[13]{0:T(128)}, s32[13]{0:T(128)S(1)}, u32[]{:S(2)}) copy-start(s32[13]{0:T(128)S(1)} %fusion.74) | copy-start | bytes 160
  346.9 78.2 %copy-start.18 = (bf16[256,2496]{0,1:T(8,128)(2,1)}, bf16[256,2496]{0,1:T(8,128)(2,1)S(1)}, u32[]{:S(2)}) copy-start(bf16[256,2496]{0,1:T(8,128)(2,1)S(1)} %convolution_convert_fusion) | copy-start | bytes 3833860
  348.1 408.3 %all-reduce.20.cloned.1.call-start = ((), (), s32[]{:S(2)}) async-start(), calls=%async_computation.4 | async-start | bytes 3276800 | tf_op jit(solution)/shard_map/psum | solution.py:167
  449.1 139.2 %copy-start.29 = (u32[32]{0:T(128)S(1)}, u32[32]{0:T(128)}, u32[]{:S(2)}) copy-start(u32[32]{0:T(128)} %constant.182) | copy-start | bytes 388
  449.2 334.5 %all-gather.11.cloned.1.call-start = ((), (), s32[]{:S(2)}) async-start(), calls=%async_computation.5 | async-start | bytes 12800000 | tf_op jit(solution)/shard_map/all_gather | solution.py:124
  449.8 379.4 %all-reduce.22.cloned.1.call-start = ((), (), s32[]{:S(2)}) async-start(), calls=%async_computation.6 | async-start | bytes 3276800 | tf_op jit(solution)/shard_map/psum | solution.py:208
  449.8 84.0 %collective-permute-start = (bf16[3200,400]{0,1:T(8,128)(2,1)}, bf16[3200,400]{0,1:T(8,128)(2,1)}, u32[]{:S(2)}, u32[]{:S(2)}) collective-permute-start(bf16[3200,400]{0,1:T(8,128)(2,1)} %param.20), channel_id=1, source_target_pairs={{0,8},{8,16},{16,24},{24,0},{1,9},{9,17},{17,25},{25,1},{2,10},{10... | collective-permute-start | bytes 7680008 | tf_op jit(solution)/shard_map/ppermute | solution.py:20
  451.3 252.4 %collective-permute-start.1 = (bf16[3200,400]{0,1:T(8,128)(2,1)}, bf16[3200,400]{0,1:T(8,128)(2,1)}, u32[]{:S(2)}, u32[]{:S(2)}) collective-permute-start(bf16[3200,400]{0,1:T(8,128)(2,1)} %param.20), channel_id=1, source_target_pairs={{0,24},{8,0},{16,8},{24,16},{1,25},{9,1},{17,9},{25,17},{2,26},{10... | collective-permute-start | bytes 7680008 | tf_op jit(solution)/shard_map/ppermute | solution.py:23
  533.8 218.1 %collective-permute-start.2 = (bf16[3200,400]{0,1:T(8,128)(2,1)}, bf16[3200,400]{0,1:T(8,128)(2,1)}, u32[]{:S(2)}, u32[]{:S(2)}) collective-permute-start(bf16[3200,400]{0,1:T(8,128)(2,1)} %collective-permute-done), channel_id=1, source_target_pairs={{0,8},{8,16},{16,24},{24,0},{1,9},{9,17},{17,25},{25,1},{2,10},{10... | collective-permute-start | bytes 7680008 | tf_op jit(solution)/shard_map/ppermute | solution.py:20
  755.4 28.3 copy-start.20
  755.4 28.3 copy-start.22
  758.1 74.1 %copy-start = (f32[1,256,1600]{1,2,0:T(8,128)}, f32[1,256,1600]{1,2,0:T(8,128)S(1)}, u32[]{:S(2)}) copy-start(f32[1,256,1600]{1,2,0:T(8,128)S(1)} %get-tuple-element.114) | copy-start | bytes 4915204
  758.3 32.9 %copy-start.11 = (bf16[1,256,1600]{1,2,0:T(8,128)(2,1)S(1)}, bf16[1,256,1600]{1,2,0:T(8,128)(2,1)}, u32[]{:S(2)}) copy-start(bf16[1,256,1600]{1,2,0:T(8,128)(2,1)} %param.21) | copy-start | bytes 2457604
  783.7 19.1 slice-start
  783.7 19.1 slice-start.1
  791.3 11.6 slice-start.2
  807.3 1061.1 %reduce-scatter.9.cloned.1.call-start = ((), (), s32[]{:S(2)}) async-start(), calls=%async_computation.7 | async-start | bytes 4259840 | tf_op jit(solution)/shard_map/reduce_scatter | solution.py:233
  807.4 11.1 copy-start.17
  881.7 1830.5 %all-reduce.24.cloned.1.call-start = ((), (), s32[]{:S(2)}) async-start(), calls=%async_computation.8 | async-start | bytes 3276800 | tf_op jit(solution)/shard_map/psum | solution.py:251
  1886.2 1392.3 %all-reduce.26.cloned.1.call-start = ((), (), s32[]{:S(2)}) async-start(), calls=%async_computation.9 | async-start | bytes 4481024 | tf_op jit(solution)/shard_map/psum | solution.py:282
  1897.6 10.8 copy-start.28
  2639.1 59.0 %collective-permute-start.3 = (bf16[60,4800]{1,0:T(8,128)(2,1)}, bf16[60,4800]{1,0:T(8,128)(2,1)}, u32[]{:S(2)}, u32[]{:S(2)}) collective-permute-start(bf16[60,4800]{1,0:T(8,128)(2,1)} %slice.41), channel_id=1, source_target_pairs={{0,2},{2,4},{4,6},{6,8},{8,10},{10,12},{12,14},{14,16},{16,18},{18... | collective-permute-start | bytes 1728008
  2650.5 23.8 copy-start.4
  2650.5 23.8 copy-start.15
  2652.8 549.9 %collective-permute-start.4 = (f32[112,3200]{1,0:T(8,128)}, f32[112,3200]{1,0:T(8,128)}, u32[]{:S(2)}, u32[]{:S(2)}) collective-permute-start(f32[112,3200]{1,0:T(8,128)} %get-tuple-element.111), channel_id=1, source_target_pairs={{0,2},{2,4},{4,6},{6,8},{8,10},{10,12},{12,14},{14,16},{16,18},{18... | collective-permute-start | bytes 4300808
  2657.0 560.3 %collective-permute-start.6 = (f32[3200,112]{0,1:T(8,128)S(1)}, f32[3200,112]{0,1:T(8,128)}, u32[]{:S(2)}, u32[]{:S(2)}) collective-permute-start(f32[3200,112]{0,1:T(8,128)S(1)} %get-tuple-element.112), channel_id=1, source_target_pairs={{0,2},{2,4},{4,6},{6,8},{8,10},{10,12},{12,14},{14,16},{16,18},{18... | collective-permute-start | bytes 4300808
  2659.5 557.8 %collective-permute-start.7 = (f32[3200,68]{0,1:T(8,128)}, f32[3200,68]{0,1:T(8,128)S(1)}, u32[]{:S(2)}, u32[]{:S(2)}) collective-permute-start(f32[3200,68]{0,1:T(8,128)} %slice.43), channel_id=1, source_target_pairs={{0,4},{2,6},{4,8},{6,10},{8,12},{10,14},{12,16},{14,18},{16,20},{1... | collective-permute-start | bytes 2611208
  2661.2 541.5 %collective-permute-start.5 = (f32[68,3200]{1,0:T(8,128)}, f32[68,3200]{1,0:T(8,128)}, u32[]{:S(2)}, u32[]{:S(2)}) collective-permute-start(f32[68,3200]{1,0:T(8,128)} %slice.42), channel_id=1, source_target_pairs={{0,4},{2,6},{4,8},{6,10},{8,12},{10,14},{12,16},{14,18},{16,20},{1... | collective-permute-start | bytes 2611208
  3234.6 43.8 %copy-start.1 = (f32[1,256,1600]{1,2,0:T(8,128)S(1)}, f32[1,256,1600]{1,2,0:T(8,128)}, u32[]{:S(2)}) copy-start(f32[1,256,1600]{1,2,0:T(8,128)} %copy-done) | copy-start | bytes 4915204
  (19 other events, 94.8 us)
Sparse Core Ops, SparseCore 0:
  9.6 269.6 all-gather.4
  280.8 97.5 all-gather.8
  380.8 44.2 all-gather.6
  449.3 20.4 all-reduce.19
  471.2 312.4 all-gather.10
  807.4 21.6 all-reduce.21
  881.8 161.7 reduce-scatter.8
  1886.3 26.6 all-reduce.23
  3202.2 76.1 all-reduce.25
